TPU v7x, 128 devices: a whole 4x4x4 slice. The times are simulated.
128 devices in a mesh: gx: 16 (over x, y), gy: 8 (over z, core).
Axes of the slice: x: 4, y: 4, z: 4, core: 2. Of those that a mesh axis runs over, the one named last changes fastest.
Arguments:
- sat_new: float32 [64, 1024, 1024], P(None, 'gx', 'gy'), may hold values from 0.02 to 1
- sat_old: float32 [64, 1024, 1024], P(None, 'gx', 'gy'), may hold values from 0.1 to 0.95
- porosity: float32 [64, 1024, 1024], P(None, 'gx', 'gy'), may hold values from 0.1 to 0.5
- spec_storage: float32 [64, 1024, 1024], P(None, 'gx', 'gy'), may hold values from 0.01 to 0.2
- pressure: float32 [64, 1024, 1024], P(None, 'gx', 'gy'), may hold values from -6 to 6
- conduct: float32 [64, 1024, 1024], P(None, 'gx', 'gy'), may hold values from 0.1 to 1
- et_rate: float32 [64, 1024, 1024], P(None, 'gx', 'gy'), may hold values from 0 to 1
- thickness: float32 [64], replicated, may hold values from 0.005 to 0.05
- labels: int32 [1024, 1024], P('gx', 'gy'), may hold values from 0 to 511, as said below
- outlet: int32 [1024, 1024], P('gx', 'gy'), may hold values 0 or 1
Outputs:
- basin_totals: float32 [4, 64, 512], replicated
- column_balance: float32 [4, 1024, 1024], P(None, 'gx', 'gy')
- peak_change: float32 [], replicated
Inputs may be any that keep to these rules, and one draw needn't show every extreme that they name: `labels`: subbasins are contiguous patches of columns with ragged edges.
All inputs are finite; a program needn't handle non-finite values. No bound on the sum of `outlet` on one device may be relied on, other than what follows from the above.
Results may differ from a plain program's by a relative error of at most 0.00016.
Values sent between devices are 32-bit elements; how exact they have to be, the bound alone decides.
A program may use at most 128 MiB of HBM per device.

v0:
```python
import jax
import jax.numpy as jnp
from jax import lax
from jax.experimental import pallas as pl
from jax.experimental.pallas import tpu as pltpu
from jax.sharding import PartitionSpec as P

SUB = 512
CH = 8
ZB = 16
MESH = pl.DeviceIdType.MESH
BF = jnp.bfloat16
F32 = jnp.float32
NT = (((1,), (1,)), ((), ()))


def split(f):
    high = f.astype(BF)
    return high, (f - high.astype(F32)).astype(BF)


def face_flow(p, k, pn, kn):
    return (k * kn) / (k + kn) * (p - pn)


def wait_all(ref, sem):
    pltpu.make_async_copy(ref, ref, sem).wait()


def make_kernel(ngx, ngy, scale):
    n = ngx * ngy

    def kernel(
        thick, labels, outlet, sn_h, so_h, po_h, ss_h, p_h, k_h, et_h,
        out, bal, top,
        sn, so, po, ss, et, p, k, depth, g, a, oh, tot, edge, halo, peak, peaks_y, peaks_x,
        pieces, own, sem_pk, sem_rest, halo_send, halo_recv, rs_send, rs_recv, ag_send, ag_recv,
        pk_send, pk_recv,
    ):
        layers, cx, cy = sn_h.shape
        chunks = cx // CH
        gx = lax.axis_index("gx")
        gy = lax.axis_index("gy")
        me = gx * ngy + gy
        barrier = pltpu.get_barrier_semaphore()

        def peer(d):
            other = lax.rem(me + d, n)
            return other, (other // ngy, lax.rem(other, ngy))

        @pl.loop(1, n)
        def _(d):
            pl.semaphore_signal(barrier, inc=1, device_id=peer(d)[1], device_id_type=MESH)

        @pl.loop(0, layers)
        def _(z):
            for i, (src, dst) in enumerate(((p_h, p), (k_h, k))):
                pltpu.make_async_copy(src.at[z], dst.at[pl.ds(0, cx), z, :], sem_pk.at[i]).start()

        rest = ((sn_h, sn), (so_h, so), (po_h, po), (ss_h, ss), (et_h, et))

        @pl.loop(0, chunks)
        def _(c):
            for r in range(CH):
                for i, (src, dst) in enumerate(rest):
                    x = c * CH + r
                    pltpu.make_async_copy(src.at[:, x, :], dst.at[x], sem_rest.at[i, c]).start()

        for z in range(layers):
            depth[pl.ds(z, 1), :] = jnp.full((1, cy), thick[z], F32)
        p[cx] = jnp.zeros((layers, cy), F32)
        k[cx] = jnp.zeros((layers, cy), F32)
        g[...] = jnp.zeros_like(g)
        peak[...] = jnp.zeros_like(peak)
        tot[...] = jnp.zeros_like(tot)
        lane = lax.broadcasted_iota(jnp.int32, (ZB, cy), 1)
        inner = lane > 0
        iota = lax.broadcasted_iota(jnp.int32, (256, cy), 0).astype(F32).astype(BF)
        one = jnp.ones((16, cy), BF)
        zero = jnp.zeros((16, cy), BF)

        def write_onehot(lab, col):
            high = lab >= 256
            low = jnp.where(high, lab - 256, lab).astype(F32)
            low = jnp.broadcast_to(low, (16, cy)).astype(BF)
            high = jnp.broadcast_to(jnp.where(high, 1.0, 0.0), (16, cy)).astype(BF)
            for r in range(16):
                e = jnp.where(iota[r * 16 : (r + 1) * 16] == low, one, zero)
                eh = e * high
                oh[pl.ds(r * 16, 16), col] = e - eh
                oh[pl.ds(256 + r * 16, 16), col] = eh

        wait_all(p.at[pl.ds(0, cx)], sem_pk.at[0])
        wait_all(k.at[pl.ds(0, cx)], sem_pk.at[1])

        lanes = lax.broadcasted_iota(jnp.int32, (layers, cy), 1)

        def take(x, carry):
            first, last = lanes == x, lanes == x + cx
            res = []
            for ref, acc in zip((p, k), carry):
                v = ref[x]
                acc = jnp.where(first, pltpu.roll(v, x, 1), acc)
                res.append(jnp.where(last, pltpu.roll(v, x + cx + 1, 1), acc))
            return tuple(res)

        e0 = jnp.zeros((layers, cy), F32)
        ep, ek = lax.fori_loop(0, cx, take, (e0, e0))
        edge[0] = ep
        edge[1] = ek

        def chunk(c):
            for i, (_, dst) in enumerate(rest):
                wait_all(dst.at[pl.ds(c * CH, CH)], sem_rest.at[i, c])

            @pl.loop(0, CH)
            def _(i):
                x = c * CH + i
                col = pl.ds(pl.multiple_of(i * cy, cy), cy)
                write_onehot(labels[pl.ds(x, 1), :], col)
                mask = outlet[pl.ds(x, 1), :].astype(F32)
                sums = [jnp.zeros((8, cy), F32)] * 4
                top_here = peak[...]
                for zb in range(layers // ZB):
                    zs = pl.ds(zb * ZB, ZB)
                    d = depth[zs, :]
                    pc, kc = p[x, zs, :], k[x, zs, :]
                    gn = face_flow(p[x + 1, zs, :], kc, pc, k[x + 1, zs, :])
                    gp = g[zs, :]
                    g[zs, :] = gn
                    h = face_flow(pc, kc, pltpu.roll(pc, 1, 1), pltpu.roll(kc, 1, 1))
                    h = jnp.where(inner, h, 0.0)
                    flux = (d + d) * (gp - gn + h - pltpu.roll(h, cy - 1, 1))
                    snv, pov = sn[x, zs, :], po[x, zs, :]
                    dif = snv - so[x, zs, :]
                    water = d * snv * (pov + ss[x, zs, :] * pc)
                    change = d * pov * dif
                    uptake = d * et[x, zs, :]
                    big = jnp.abs(dif)
                    top_here = jnp.maximum(top_here, jnp.maximum(big[:8], big[8:]))
                    for q, f in enumerate((water, change, uptake, flux)):
                        sums[q] = sums[q] + (f[:8] + f[8:])
                        high, low = split(f * mask if q == 3 else f)
                        a[pl.ds(q * layers + zb * ZB, ZB), col] = high
                        a[pl.ds((4 + q) * layers + zb * ZB, ZB), col] = low
                peak[...] = top_here
                for q in range(4):
                    bal[q, pl.ds(x, 1), :] = jnp.sum(sums[q], axis=0, keepdims=True)

            r = lax.dot_general(a[...], oh[...], NT, preferred_element_type=F32)
            tot[...] += r[: 4 * layers] + r[4 * layers :]

        half = chunks // 2

        @pl.loop(0, half)
        def _(c):
            chunk(c)

        pl.semaphore_wait(barrier, n - 1)

        def halo_copy(src, slot, ox, oy):
            to = (lax.rem(gx + ox + ngx, ngx), lax.rem(gy + oy + ngy, ngy))
            return pltpu.make_async_remote_copy(
                src_ref=src, dst_ref=halo.at[slot], send_sem=halo_send.at[slot],
                recv_sem=halo_recv.at[slot], device_id=to, device_id_type=MESH,
            )

        halos = []
        for i, ref in enumerate((p, k)):
            halos.append(halo_copy(ref.at[cx - 1], i, 1, 0))
            halos.append(halo_copy(ref.at[0], 2 + i, -1, 0))
            halos.append(halo_copy(edge.at[i], 4 + i, 0, 1))
            halos.append(halo_copy(edge.at[i], 6 + i, 0, -1))
        for h in halos:
            h.start()

        @pl.loop(half, chunks)
        def _(c):
            chunk(c)

        for h in halos:
            h.wait()
        left = lanes < cx
        ly = jnp.concatenate([labels[...]] * 2, axis=0).astype(F32).T
        oy = jnp.concatenate([outlet[...]] * 2, axis=0).astype(F32).T
        first = lax.broadcasted_iota(jnp.int32, (1, cy), 1) < cx
        lab_y = jnp.where(first, ly[:1], ly[cy - 1 :]).astype(jnp.int32)
        out_y = jnp.where(first, oy[:1], oy[cy - 1 :])
        d2 = depth[...] + depth[...]
        py = jnp.where(left, pltpu.roll(halo[4], cx, 1), pltpu.roll(halo[6], cx, 1))
        ky = jnp.where(left, pltpu.roll(halo[5], cx, 1), pltpu.roll(halo[7], cx, 1))
        inside = jnp.where(left, jnp.where(gy > 0, 1.0, 0.0), jnp.where(gy < ngy - 1, 1.0, 0.0))
        borders = (
            (p[0], k[0], halo[0], halo[1] * jnp.where(gx > 0, 1.0, 0.0), labels[:1, :], outlet[:1, :].astype(F32)),
            (
                p[cx - 1], k[cx - 1], halo[2], halo[3] * jnp.where(gx < ngx - 1, 1.0, 0.0),
                labels[cx - 1 :, :], outlet[cx - 1 :, :].astype(F32),
            ),
            (edge[0], edge[1], py, ky * inside, lab_y, out_y),
        )
        for i, (pc, kc, pn, kn, lab, mask) in enumerate(borders):
            f = d2 * face_flow(pc, kc, pn, kn)
            col = pl.ds(i * cy, cy)
            write_onehot(lab, col)
            high, low = split(f * mask)
            a[pl.ds(0, layers), col] = high
            a[pl.ds(layers, layers), col] = low
            f = jnp.sum(f, axis=0, keepdims=True)
            if i < 2:
                x = i * (cx - 1)
                bal[3, x : x + 1, :] += f
            else:
                ft = jnp.broadcast_to(f, (8, cy)).T
                at = lax.broadcasted_iota(jnp.int32, (cx, cy), 1)
                low_side = jnp.where(at == 0, jnp.broadcast_to(ft[:cx, :1], (cx, cy)), 0.0)
                high_side = jnp.where(at == cy - 1, jnp.broadcast_to(ft[cx:, :1], (cx, cy)), 0.0)
                bal[3] += low_side + high_side
        r = lax.dot_general(
            a[: 2 * layers, : 3 * cy], oh[:, : 3 * cy], NT, preferred_element_type=F32
        )
        tot[pl.ds(3 * layers, layers), :] += r[:layers] + r[layers:]

        def peak_copy(src, dst, send, recv, to):
            return pltpu.make_async_remote_copy(
                src_ref=src, dst_ref=dst, send_sem=send, recv_sem=recv, device_id=to, device_id_type=MESH
            )

        @pl.loop(1, ngy)
        def _(d):
            to = (gx, lax.rem(gy + d, ngy))
            peak_copy(peak, peaks_y.at[d - 1], pk_send.at[0], pk_recv.at[0], to).start()

        def tile(ref, owner):
            per_row = SUB // 128
            row = pl.multiple_of(owner // per_row * 8, 8)
            colt = pl.multiple_of(lax.rem(owner, per_row) * 128, 128)
            return ref.at[pl.ds(row, 8), pl.ds(colt, 128)]

        @pl.loop(1, n)
        def _(d):
            other, to = peer(d)
            peak_copy(tile(tot, other), pieces.at[d - 1], rs_send, rs_recv, to).start()

        wait_all(peaks_y, pk_recv.at[0])
        wait_all(peaks_y, pk_send.at[0])
        best = peak[...]
        for d in range(ngy - 1):
            best = jnp.maximum(best, peaks_y[d])
        peak[...] = best

        @pl.loop(1, ngx)
        def _(d):
            to = (lax.rem(gx + d, ngx), gy)
            peak_copy(peak, peaks_x.at[d - 1], pk_send.at[1], pk_recv.at[1], to).start()

        wait_all(pieces, rs_recv)
        total = tile(tot, me)[...]
        for d in range(n - 1):
            total = total + pieces[d]
        own[...] = total * scale

        @pl.loop(1, n)
        def _(d):
            _, to = peer(d)
            peak_copy(own, tile(out, me), ag_send, ag_recv, to).start()

        tile(out, me)[...] = own[...]
        wait_all(peaks_x, pk_recv.at[1])
        wait_all(peaks_x, pk_send.at[1])
        best = peak[...]
        for d in range(ngx - 1):
            best = jnp.maximum(best, peaks_x[d])
        top[0] = jnp.max(best)
        wait_all(pieces, rs_send)
        wait_all(pieces, ag_recv)
        wait_all(pieces, ag_send)

    return kernel


def solution(mesh):
    ngx, ngy = mesh.shape["gx"], mesh.shape["gy"]
    n = ngx * ngy

    def on_device(sat_new, sat_old, porosity, spec_storage, pressure, conduct, et_rate, thickness, labels, outlet):
        layers, cx, cy = sat_new.shape
        scale = layers * SUB / (ngx * cx * ngy * cy)
        field = pltpu.VMEM((cx, layers, cy), F32)
        longer = pltpu.VMEM((cx + 1, layers, cy), F32)
        sheet = pltpu.VMEM((layers, cy), F32)
        dma = pltpu.SemaphoreType.DMA
        vm = pl.BlockSpec(memory_space=pltpu.VMEM)
        out, bal, top = pl.pallas_call(
            make_kernel(ngx, ngy, scale),
            out_shape=(
                jax.ShapeDtypeStruct((4 * layers, SUB), F32),
                jax.ShapeDtypeStruct((4, cx, cy), F32),
                jax.ShapeDtypeStruct((1,), F32),
            ),
            in_specs=[pl.BlockSpec(memory_space=pltpu.SMEM), vm, vm] + [pl.BlockSpec(memory_space=pl.ANY)] * 7,
            out_specs=(vm, vm, pl.BlockSpec(memory_space=pltpu.SMEM)),
            scratch_shapes=[
                field, field, field, field, field, longer, longer,
                sheet,
                sheet,
                pltpu.VMEM((8 * layers, CH * cy), BF),
                pltpu.VMEM((SUB, CH * cy), BF),
                pltpu.VMEM((4 * layers, SUB), F32),
                pltpu.VMEM((2, layers, cy), F32),
                pltpu.VMEM((8, layers, cy), F32),
                pltpu.VMEM((8, cy), F32),
                pltpu.VMEM((ngy - 1, 8, cy), F32),
                pltpu.VMEM((ngx - 1, 8, cy), F32),
                pltpu.VMEM((n - 1, 8, 128), F32),
                pltpu.VMEM((8, 128), F32),
                dma((2,)), dma((5, cx // CH)), dma((8,)), dma((8,)), dma, dma, dma, dma, dma((2,)), dma((2,)),
            ],
            compiler_params=pltpu.CompilerParams(
                collective_id=0, has_side_effects=True, vmem_limit_bytes=60 << 20
            ),
            name="balance",
        )(thickness, labels, outlet, sat_new, sat_old, porosity, spec_storage, pressure, conduct, et_rate)
        return out.reshape(4, layers, SUB), bal, top.reshape(())

    cells = P(None, "gx", "gy")
    return jax.shard_map(
        on_device,
        mesh=mesh,
        in_specs=(cells,) * 7 + (P(), P("gx", "gy"), P("gx", "gy")),
        out_specs=(P(), cells, P()),
        check_vma=False,
    )
```

profile of v0, /device:TPU:1, one launch (start us, length us, event | category | flops | bytes accessed | tf_op | source)
XLA Modules:
  0.0 62.9 jit_solution(5093167719917626749)
XLA Ops:
  0.6 57.1 %balance.1 = (f32[256,512]{1,0:T(8,128)}, f32[4,64,128]{2,1,0:T(8,128)}, f32[1]{0:T(128)}) custom-call(f32[64]{0:T(128)} %thick.1, s32[64,128]{1,0:T(8,128)} %labels.1, s32[64,128]{1,0:T(8,128)} %outlet.1, f32[64,64,128]{2,1,0:T(8,128)} %sn_h.1, f32[64,64,128]{2,1,0:T(8,128)} %so_h.1, f32[64,64,128]{2,1,0:T(8,128)} %po_h.1, f32[64,64,128]{2,1,0:T(8,128)} %ss_h.1, ...), custom_call_target="tpu_custom_call" | custom-call | tf_op jit(solution)/shard_map/balance/pallas_call | solution.py:293
  57.7 1.9 %copy.16 = f32[4,64,512]{2,1,0:T(8,128)} copy(f32[4,64,512]{2,1,0:T(8,128)} %bitcast.2) | data formatting | bytes 1048576
  59.6 1.6 %copy.17 = f32[4,64,128]{2,1,0:T(8,128)} copy(f32[4,64,128]{2,1,0:T(8,128)} %get-tuple-element.13) | data formatting | bytes 262144
where the time goes:
time: 63.2 us; the launch traced here: 62.9 us
  Pallas kernels  57.1 us (90%)
  local copies, waits for them, and re-layouts  3.44 us (5%)
  between operations  2.39 us (4%)
    pallas_call x1, Pallas kernels, on_device(): pl.pallas_call(make_kernel(ngx, ngy, scale), out_shape=(jax.ShapeDtypeStr...  57.1 us
    unnamed x2, local copies, waits for them, and re-layouts  3.44 us

commit v1 on v0

v1 whole, which is shorter than its diff:
```python
import jax
import jax.numpy as jnp
from jax import lax
from jax.experimental import pallas as pl
from jax.experimental.pallas import tpu as pltpu
from jax.sharding import PartitionSpec as P

SUB = 512
NP = 4
ZB = 16
MESH = pl.DeviceIdType.MESH
BF = jnp.bfloat16
F32 = jnp.float32
NT = (((1,), (1,)), ((), ()))


def split(f):
    high = f.astype(BF)
    return high, (f - high.astype(F32)).astype(BF)


def face_flow(p, k, pn, kn):
    return (k * kn) / (k + kn) * (p - pn)


def wait_all(ref, sem):
    pltpu.make_async_copy(ref, ref, sem).wait()


def make_kernel(ngx, ngy, scale):
    chips_y = ngy // 2
    n = ngx * ngy

    def kernel(
        thick_h, labels_h, outlet_h, sn_h, so_h, po_h, ss_h, p_h, k_h, et_h,
        out, bal_h, top,
        thick, labels, outlet, sn, so, po, ss, et, p, k, depth, g, a0, a1, oh0, oh1, tot, half, whole, bal,
        edge, halo, peak, peaks_y, peaks_x, pieces, own,
        sem_small, sem_pk, sem_rest, halo_send, halo_recv, pair_send, pair_recv,
        rs_send, rs_recv, ag_send, ag_recv, pk_send, pk_recv, sem_out,
    ):
        layers, cx, cy = sn_h.shape
        per = 2 * NP
        turns = cx // per
        gx = lax.axis_index("gx")
        gy = lax.axis_index("gy")
        chip = gy // 2
        core = gy - chip * 2
        barrier = pltpu.get_barrier_semaphore()

        def wrap(v, m):
            return jnp.where(v >= m, v - m, v)

        smalls = ((thick_h, thick), (labels_h, labels), (outlet_h, outlet))
        for i, (src, dst) in enumerate(smalls):
            pltpu.make_async_copy(src, dst, sem_small.at[i]).start()

        @pl.loop(0, layers)
        def _(z):
            for i, (src, dst) in enumerate(((p_h, p), (k_h, k))):
                pltpu.make_async_copy(src.at[z], dst.at[pl.ds(0, cx), z, :], sem_pk.at[i]).start()

        rest = ((sn_h, sn), (so_h, so), (po_h, po), (ss_h, ss), (et_h, et))

        @pl.loop(0, turns)
        def _(c):
            for r in range(per):
                for i, (src, dst) in enumerate(rest):
                    x = c * per + r
                    pltpu.make_async_copy(src.at[:, x, :], dst.at[x], sem_rest.at[i, c]).start()

        chips = [wrap(chip + d, chips_y) for d in range(chips_y)]

        def each_chip(f):
            for d in range(1, chips_y):
                f(d - 1, gx, chips[d])

            @pl.loop(1, ngx)
            def _(i):
                at = wrap(gx + i, ngx)
                for d in range(chips_y):
                    f(i * chips_y + d - 1, at, chips[d])

        def greet(to):
            pl.semaphore_signal(barrier, inc=1, device_id=to, device_id_type=MESH)

        partner = (gx, chip * 2 + 1 - core)
        greet(partner)
        each_chip(lambda i, x, z: greet((x, z * 2 + core)))
        for d in range(1, chips_y):
            greet((gx, chips[d] * 2 + 1 - core))

        for (src, dst), i in zip(smalls, range(3)):
            pltpu.make_async_copy(src, dst, sem_small.at[i]).wait()
        for z in range(layers):
            depth[pl.ds(z, 1), :] = jnp.full((1, cy), thick[z], F32)
        p[cx] = jnp.zeros((layers, cy), F32)
        k[cx] = jnp.zeros((layers, cy), F32)
        g[...] = jnp.zeros_like(g)
        peak[...] = jnp.zeros_like(peak)
        tot[...] = jnp.zeros_like(tot)
        a1[...] = jnp.zeros_like(a1)
        oh1[...] = jnp.zeros_like(oh1)
        lane = lax.broadcasted_iota(jnp.int32, (ZB, cy), 1)
        inner = lane > 0
        iota = lax.broadcasted_iota(jnp.int32, (256, cy), 0).astype(F32).astype(BF)
        one = jnp.ones((16, cy), BF)
        zero = jnp.zeros((16, cy), BF)

        def write_onehot(oh, lab, col):
            high = lab >= 256
            low = jnp.where(high, lab - 256, lab).astype(F32)
            low = jnp.broadcast_to(low, (16, cy)).astype(BF)
            high = jnp.broadcast_to(jnp.where(high, 1.0, 0.0), (16, cy)).astype(BF)
            for r in range(16):
                e = jnp.where(iota[r * 16 : (r + 1) * 16] == low, one, zero)
                eh = e * high
                oh[r * 16 : r * 16 + 16, col] = e - eh
                oh[256 + r * 16 : 272 + r * 16, col] = eh

        wait_all(p.at[pl.ds(0, cx)], sem_pk.at[0])
        wait_all(k.at[pl.ds(0, cx)], sem_pk.at[1])

        lanes = lax.broadcasted_iota(jnp.int32, (layers, cy), 1)

        def take(x, carry):
            first, last = lanes == x, lanes == x + cx
            res = []
            for ref, acc in zip((p, k), carry):
                v = ref[x]
                acc = jnp.where(first, pltpu.roll(v, x, 1), acc)
                res.append(jnp.where(last, pltpu.roll(v, x + cx + 1, 1), acc))
            return tuple(res)

        e0 = jnp.zeros((layers, cy), F32)
        ep, ek = lax.fori_loop(0, cx, take, (e0, e0))
        edge[0] = ep
        edge[1] = ek

        def fields(x, a, oh, j):
            col = slice(j * cy, (j + 1) * cy)
            write_onehot(oh, labels[pl.ds(x, 1), :], col)
            mask = outlet[pl.ds(x, 1), :].astype(F32)
            sums = [jnp.zeros((8, cy), F32)] * 4
            top_here = peak[...]
            for zb in range(layers // ZB):
                zs = pl.ds(zb * ZB, ZB)
                d = depth[zs, :]
                pc, kc = p[x, zs, :], k[x, zs, :]
                gn = face_flow(p[x + 1, zs, :], kc, pc, k[x + 1, zs, :])
                gp = g[zs, :]
                g[zs, :] = gn
                h = face_flow(pc, kc, pltpu.roll(pc, 1, 1), pltpu.roll(kc, 1, 1))
                h = jnp.where(inner, h, 0.0)
                flux = (d + d) * (gp - gn + h - pltpu.roll(h, cy - 1, 1))
                snv, pov = sn[x, zs, :], po[x, zs, :]
                dif = snv - so[x, zs, :]
                water = d * snv * (pov + ss[x, zs, :] * pc)
                change = d * pov * dif
                uptake = d * et[x, zs, :]
                big = jnp.abs(dif)
                top_here = jnp.maximum(top_here, jnp.maximum(big[:8], big[8:]))
                for q, f in enumerate((water, change, uptake, flux)):
                    sums[q] = sums[q] + (f[:8] + f[8:])
                    high, low = split(f * mask if q == 3 else f)
                    r0 = q * layers + zb * ZB
                    a[r0 : r0 + ZB, col] = high
                    a[4 * layers + r0 : 4 * layers + r0 + ZB, col] = low
            peak[...] = top_here
            for q in range(4):
                bal[q, pl.ds(x, 1), :] = jnp.sum(sums[q], axis=0, keepdims=True)

        def product(a, oh):
            r = lax.dot_general(a[...], oh[...], NT, preferred_element_type=F32)
            tot[...] += r[: 4 * layers] + r[4 * layers :]

        def turns_of(begin, end):
            @pl.loop(begin, end)
            def _(c):
                for i, (_, dst) in enumerate(rest):
                    wait_all(dst.at[pl.ds(c * per, per)], sem_rest.at[i, c])
                product(a1, oh1)
                for j in range(NP):
                    fields(c * per + j, a0, oh0, j)
                product(a0, oh0)
                for j in range(NP):
                    fields(c * per + NP + j, a1, oh1, j)

        def send(src, dst, send_sem, recv_sem, to):
            copy = pltpu.make_async_remote_copy(
                src_ref=src, dst_ref=dst, send_sem=send_sem, recv_sem=recv_sem, device_id=to, device_id_type=MESH
            )
            copy.start()
            return copy

        turns_of(0, turns // 2)
        pl.semaphore_wait(barrier, (ngx + 1) * chips_y - 1)

        x_next, x_last = wrap(gx + 1, ngx), wrap(gx + ngx - 1, ngx)
        y_next, y_last = wrap(gy + 1, ngy), wrap(gy + ngy - 1, ngy)
        halos = []
        for i, ref in enumerate((p, k)):
            for slot, src, to in (
                (i, ref.at[cx - 1], (x_next, gy)),
                (2 + i, ref.at[0], (x_last, gy)),
                (4 + i, edge.at[i], (gx, y_next)),
                (6 + i, edge.at[i], (gx, y_last)),
            ):
                halos.append(send(src, halo.at[slot], halo_send.at[slot], halo_recv.at[slot], to))

        turns_of(turns // 2, turns)
        product(a1, oh1)

        chips8 = [wrap(gy + d, ngy) for d in range(1, ngy)]
        for d in range(ngy - 1):
            send(peak, peaks_y.at[d], pk_send.at[0], pk_recv.at[0], (gx, chips8[d]))

        for h in halos:
            h.wait()
        left = lanes < cx
        ly = jnp.concatenate([labels[...]] * 2, axis=0).astype(F32).T
        oy = jnp.concatenate([outlet[...]] * 2, axis=0).astype(F32).T
        first = lax.broadcasted_iota(jnp.int32, (1, cy), 1) < cx
        lab_y = jnp.where(first, ly[:1], ly[cy - 1 :]).astype(jnp.int32)
        out_y = jnp.where(first, oy[:1], oy[cy - 1 :])
        d2 = depth[...] + depth[...]
        py = jnp.where(left, pltpu.roll(halo[4], cx, 1), pltpu.roll(halo[6], cx, 1))
        ky = jnp.where(left, pltpu.roll(halo[5], cx, 1), pltpu.roll(halo[7], cx, 1))
        inside = jnp.where(left, jnp.where(gy > 0, 1.0, 0.0), jnp.where(gy < ngy - 1, 1.0, 0.0))
        borders = (
            (p[0], k[0], halo[0], halo[1] * jnp.where(gx > 0, 1.0, 0.0), labels[:1, :], outlet[:1, :].astype(F32)),
            (
                p[cx - 1], k[cx - 1], halo[2], halo[3] * jnp.where(gx < ngx - 1, 1.0, 0.0),
                labels[cx - 1 :, :], outlet[cx - 1 :, :].astype(F32),
            ),
            (edge[0], edge[1], py, ky * inside, lab_y, out_y),
        )
        for i, (pc, kc, pn, kn, lab, mask) in enumerate(borders):
            f = d2 * face_flow(pc, kc, pn, kn)
            col = slice(i * cy, (i + 1) * cy)
            write_onehot(oh0, lab, col)
            high, low = split(f * mask)
            a0[:layers, col] = high
            a0[layers : 2 * layers, col] = low
            f = jnp.sum(f, axis=0, keepdims=True)
            if i < 2:
                x = i * (cx - 1)
                bal[3, x : x + 1, :] += f
            else:
                ft = jnp.broadcast_to(f, (8, cy)).T
                at = lax.broadcasted_iota(jnp.int32, (cx, cy), 1)
                low_side = jnp.where(at == 0, jnp.broadcast_to(ft[:cx, :1], (cx, cy)), 0.0)
                high_side = jnp.where(at == cy - 1, jnp.broadcast_to(ft[cx:, :1], (cx, cy)), 0.0)
                bal[3] += low_side + high_side
        r = lax.dot_general(
            a0[: 2 * layers, : 3 * cy], oh0[:, : 3 * cy], NT, preferred_element_type=F32
        )
        tot[pl.ds(3 * layers, layers), :] += r[:layers] + r[layers:]

        rows = 2 * layers
        mine, theirs = (pl.multiple_of(v * rows, rows) for v in (core, 1 - core))
        pair = send(tot.at[pl.ds(theirs, rows), :], half, pair_send.at[0], pair_recv.at[0], partner)
        bal_copy = pltpu.make_async_copy(bal, bal_h, sem_out.at[0])
        bal_copy.start()

        wait_all(peaks_y, pk_recv.at[0])
        wait_all(peaks_y, pk_send.at[0])
        best = peak[...]
        for d in range(ngy - 1):
            best = jnp.maximum(best, peaks_y[d])
        peak[...] = best

        pair.wait()
        tot[pl.ds(mine, rows), :] += half[...]

        def tile(ref, x, z):
            return ref.at[
                pl.ds(pl.multiple_of(core * rows + x * 8, 8), 8), pl.ds(pl.multiple_of(z * 128, 128), 128)
            ]

        each_chip(lambda i, x, z: send(tile(tot, x, z), pieces.at[i], rs_send, rs_recv, (x, z * 2 + core)))

        @pl.loop(1, ngx)
        def _(d):
            send(peak, peaks_x.at[d - 1], pk_send.at[1], pk_recv.at[1], (wrap(gx + d, ngx), gy))

        wait_all(pieces, rs_recv)
        terms = [tile(tot, gx, chip)[...]] + [pieces[d] for d in range(n // 2 - 1)]
        while len(terms) > 1:
            terms = [a + b for a, b in zip(terms[::2], terms[1::2])] + terms[len(terms) // 2 * 2 :]
        own[...] = terms[0] * scale

        here = tile(whole, gx, chip)
        each_chip(lambda i, x, z: send(own, here, ag_send, ag_recv, (x, z * 2 + core)))
        here[...] = own[...]
        wait_all(peaks_x, pk_recv.at[1])
        wait_all(peaks_x, pk_send.at[1])
        best = peak[...]
        for d in range(ngx - 1):
            best = jnp.maximum(best, peaks_x[d])
        top[0] = jnp.max(best)
        bal_copy.wait()
        wait_all(pieces, rs_send)
        wait_all(pieces, ag_recv)
        done = whole.at[pl.ds(mine, rows), :]
        pair = send(done, out.at[pl.ds(mine, rows), :], pair_send.at[1], pair_recv.at[1], partner)
        out_copy = pltpu.make_async_copy(done, out.at[pl.ds(mine, rows), :], sem_out.at[1])
        out_copy.start()
        wait_all(pieces, ag_send)
        out_copy.wait()
        pair.wait()

    return kernel


def solution(mesh):
    ngx, ngy = mesh.shape["gx"], mesh.shape["gy"]
    n = ngx * ngy

    def on_device(sat_new, sat_old, porosity, spec_storage, pressure, conduct, et_rate, thickness, labels, outlet):
        layers, cx, cy = sat_new.shape
        scale = layers * SUB / (ngx * cx * ngy * cy)
        field = pltpu.VMEM((cx, layers, cy), F32)
        longer = pltpu.VMEM((cx + 1, layers, cy), F32)
        sheet = pltpu.VMEM((layers, cy), F32)
        dma = pltpu.SemaphoreType.DMA
        anywhere = pl.BlockSpec(memory_space=pl.ANY)
        out, bal, top = pl.pallas_call(
            make_kernel(ngx, ngy, scale),
            out_shape=(
                jax.ShapeDtypeStruct((4 * layers, SUB), F32),
                jax.ShapeDtypeStruct((4, cx, cy), F32),
                jax.ShapeDtypeStruct((1,), F32),
            ),
            in_specs=[anywhere] * 10,
            out_specs=(anywhere, anywhere, pl.BlockSpec(memory_space=pltpu.SMEM)),
            scratch_shapes=[
                pltpu.SMEM((layers,), F32),
                pltpu.VMEM((cx, cy), jnp.int32),
                pltpu.VMEM((cx, cy), jnp.int32),
                field, field, field, field, field, longer, longer,
                sheet,
                sheet,
                pltpu.VMEM((8 * layers, NP * cy), BF),
                pltpu.VMEM((8 * layers, NP * cy), BF),
                pltpu.VMEM((SUB, NP * cy), BF),
                pltpu.VMEM((SUB, NP * cy), BF),
                pltpu.VMEM((4 * layers, SUB), F32),
                pltpu.VMEM((2 * layers, SUB), F32),
                pltpu.VMEM((4 * layers, SUB), F32),
                pltpu.VMEM((4, cx, cy), F32),
                pltpu.VMEM((2, layers, cy), F32),
                pltpu.VMEM((8, layers, cy), F32),
                pltpu.VMEM((8, cy), F32),
                pltpu.VMEM((ngy - 1, 8, cy), F32),
                pltpu.VMEM((ngx - 1, 8, cy), F32),
                pltpu.VMEM((n // 2 - 1, 8, 128), F32),
                pltpu.VMEM((8, 128), F32),
                dma((3,)), dma((2,)), dma((5, cx // (2 * NP))), dma((8,)), dma((8,)), dma((2,)), dma((2,)),
                dma, dma, dma, dma, dma((2,)), dma((2,)), dma((2,)),
            ],
            compiler_params=pltpu.CompilerParams(
                collective_id=0, has_side_effects=True, vmem_limit_bytes=60 << 20
            ),
            name="balance",
        )(thickness, labels, outlet, sat_new, sat_old, porosity, spec_storage, pressure, conduct, et_rate)
        return out.reshape(4, layers, SUB), bal, top.reshape(())

    cells = P(None, "gx", "gy")
    return jax.shard_map(
        on_device,
        mesh=mesh,
        in_specs=(cells,) * 7 + (P(), P("gx", "gy"), P("gx", "gy")),
        out_specs=(P(), cells, P()),
        check_vma=False,
    )
```

time: 63.2 us -> 48.6 us (0.77)
  Pallas kernels: 57.1 us -> 42.5 us
    pallas_call x1, Pallas kernels: 57.1 us -> 42.5 us  [on_device(): pl.pallas_call(make_kernel(ngx, ngy, scale), out_shape=(jax.ShapeDtypeStr...]
where the time goes in v1:
time: 48.6 us; the launch traced here: 48.4 us
  Pallas kernels  42.5 us (87%)
  local copies, waits for them, and re-layouts  3.44 us (7%)
  between operations  2.39 us (5%)
    pallas_call x1, Pallas kernels, on_device(): pl.pallas_call(make_kernel(ngx, ngy, scale), out_shape=(jax.ShapeDtypeStr...  42.5 us
    unnamed x2, local copies, waits for them, and re-layouts  3.44 us

profile of v1, /device:TPU:1, one launch (start us, length us, event | category | flops | bytes accessed | tf_op | source)
XLA Modules:
  0.0 48.4 jit_solution(18006351433832694418)
XLA Ops:
  0.6 42.5 %balance.1 = (f32[256,512]{1,0:T(8,128)}, f32[4,64,128]{2,1,0:T(8,128)}, f32[1]{0:T(128)}) custom-call(f32[64]{0:T(128)} %thick_h.1, s32[64,128]{1,0:T(8,128)} %labels_h.1, s32[64,128]{1,0:T(8,128)} %outlet_h.1, f32[64,64,128]{2,1,0:T(8,128)} %sn_h.1, f32[64,64,128]{2,1,0:T(8,128)} %so_h.1, f32[64,64,128]{2,1,0:T(8,128)} %po_h.1, f32[64,64,128]{2,1,0:T(8,128)} %ss_h.1, ...), custom_call_target="tpu_custom_call" | custom-call | tf_op jit(solution)/shard_map/balance/pallas_call | solution.py:328
  43.2 1.9 %copy.16 = f32[4,64,512]{2,1,0:T(8,128)} copy(f32[4,64,512]{2,1,0:T(8,128)} %bitcast.2) | data formatting | bytes 1048576
  45.1 1.6 %copy.17 = f32[4,64,128]{2,1,0:T(8,128)} copy(f32[4,64,128]{2,1,0:T(8,128)} %get-tuple-element.13) | data formatting | bytes 262144

commit v2 on v1

--- a/solution.py
+++ b/solution.py
@@ -34,7 +34,7 @@
     def kernel(
         thick_h, labels_h, outlet_h, sn_h, so_h, po_h, ss_h, p_h, k_h, et_h,
         out, bal_h, top,
-        thick, labels, outlet, sn, so, po, ss, et, p, k, depth, g, a0, a1, oh0, oh1, tot, half, whole, bal,
+        thick, labels, outlet, sn, so, po, ss, et, p, k, depth, g, a0, a1, oh0, oh1, tot, half, bal,
         edge, halo, peak, peaks_y, peaks_x, pieces, own,
         sem_small, sem_pk, sem_rest, halo_send, halo_recv, pair_send, pair_recv,
         rs_send, rs_recv, ag_send, ag_recv, pk_send, pk_recv, sem_out,
@@ -51,6 +51,27 @@
         def wrap(v, m):
             return jnp.where(v >= m, v - m, v)
 
+        chips = [wrap(chip + d, chips_y) for d in range(chips_y)]
+
+        def each_chip(f):
+            for d in range(1, chips_y):
+                f(d - 1, gx, chips[d])
+
+            @pl.loop(1, ngx)
+            def _(i):
+                at = wrap(gx + i, ngx)
+                for d in range(chips_y):
+                    f(i * chips_y + d - 1, at, chips[d])
+
+        def greet(to):
+            pl.semaphore_signal(barrier, inc=1, device_id=to, device_id_type=MESH)
+
+        partner = (gx, chip * 2 + 1 - core)
+        greet(partner)
+        each_chip(lambda i, x, z: greet((x, z * 2 + core)))
+        for d in range(1, chips_y):
+            greet((gx, chips[d] * 2 + 1 - core))
+
         smalls = ((thick_h, thick), (labels_h, labels), (outlet_h, outlet))
         for i, (src, dst) in enumerate(smalls):
             pltpu.make_async_copy(src, dst, sem_small.at[i]).start()
@@ -68,27 +89,6 @@
                 for i, (src, dst) in enumerate(rest):
                     x = c * per + r
                     pltpu.make_async_copy(src.at[:, x, :], dst.at[x], sem_rest.at[i, c]).start()
-
-        chips = [wrap(chip + d, chips_y) for d in range(chips_y)]
-
-        def each_chip(f):
-            for d in range(1, chips_y):
-                f(d - 1, gx, chips[d])
-
-            @pl.loop(1, ngx)
-            def _(i):
-                at = wrap(gx + i, ngx)
-                for d in range(chips_y):
-                    f(i * chips_y + d - 1, at, chips[d])
-
-        def greet(to):
-            pl.semaphore_signal(barrier, inc=1, device_id=to, device_id_type=MESH)
-
-        partner = (gx, chip * 2 + 1 - core)
-        greet(partner)
-        each_chip(lambda i, x, z: greet((x, z * 2 + core)))
-        for d in range(1, chips_y):
-            greet((gx, chips[d] * 2 + 1 - core))
 
         for (src, dst), i in zip(smalls, range(3)):
             pltpu.make_async_copy(src, dst, sem_small.at[i]).wait()
@@ -123,17 +123,19 @@
 
         lanes = lax.broadcasted_iota(jnp.int32, (layers, cy), 1)
 
-        def take(x, carry):
-            first, last = lanes == x, lanes == x + cx
-            res = []
-            for ref, acc in zip((p, k), carry):
-                v = ref[x]
-                acc = jnp.where(first, pltpu.roll(v, x, 1), acc)
-                res.append(jnp.where(last, pltpu.roll(v, x + cx + 1, 1), acc))
-            return tuple(res)
+        def take(t, carry):
+            for x in (4 * t, 4 * t + 1, 4 * t + 2, 4 * t + 3):
+                first, last = lanes == x, lanes == x + cx
+                res = []
+                for ref, acc in zip((p, k), carry):
+                    v = ref[x]
+                    acc = jnp.where(first, pltpu.roll(v, x, 1), acc)
+                    res.append(jnp.where(last, pltpu.roll(v, x + cx + 1, 1), acc))
+                carry = tuple(res)
+            return carry
 
         e0 = jnp.zeros((layers, cy), F32)
-        ep, ek = lax.fori_loop(0, cx, take, (e0, e0))
+        ep, ek = lax.fori_loop(0, cx // 4, take, (e0, e0))
         edge[0] = ep
         edge[1] = ek
 
@@ -290,9 +292,10 @@
             terms = [a + b for a, b in zip(terms[::2], terms[1::2])] + terms[len(terms) // 2 * 2 :]
         own[...] = terms[0] * scale
 
-        here = tile(whole, gx, chip)
+        here = tile(out, gx, chip)
         each_chip(lambda i, x, z: send(own, here, ag_send, ag_recv, (x, z * 2 + core)))
-        here[...] = own[...]
+        own_copy = pltpu.make_async_copy(own, here, sem_out.at[1])
+        own_copy.start()
         wait_all(peaks_x, pk_recv.at[1])
         wait_all(peaks_x, pk_send.at[1])
         best = peak[...]
@@ -302,12 +305,10 @@
         bal_copy.wait()
         wait_all(pieces, rs_send)
         wait_all(pieces, ag_recv)
-        done = whole.at[pl.ds(mine, rows), :]
-        pair = send(done, out.at[pl.ds(mine, rows), :], pair_send.at[1], pair_recv.at[1], partner)
-        out_copy = pltpu.make_async_copy(done, out.at[pl.ds(mine, rows), :], sem_out.at[1])
-        out_copy.start()
+        own_copy.wait()
+        done = out.at[pl.ds(mine, rows), :]
+        pair = send(done, done, pair_send.at[1], pair_recv.at[1], partner)
         wait_all(pieces, ag_send)
-        out_copy.wait()
         pair.wait()
 
     return kernel
@@ -332,7 +333,7 @@
                 jax.ShapeDtypeStruct((4, cx, cy), F32),
                 jax.ShapeDtypeStruct((1,), F32),
             ),
-            in_specs=[anywhere] * 10,
+            in_specs=[pl.BlockSpec(memory_space=pltpu.HBM)] * 10,
             out_specs=(anywhere, anywhere, pl.BlockSpec(memory_space=pltpu.SMEM)),
             scratch_shapes=[
                 pltpu.SMEM((layers,), F32),
@@ -347,7 +348,6 @@
                 pltpu.VMEM((SUB, NP * cy), BF),
                 pltpu.VMEM((4 * layers, SUB), F32),
                 pltpu.VMEM((2 * layers, SUB), F32),
-                pltpu.VMEM((4 * layers, SUB), F32),
                 pltpu.VMEM((4, cx, cy), F32),
                 pltpu.VMEM((2, layers, cy), F32),
                 pltpu.VMEM((8, layers, cy), F32),
@@ -360,10 +360,13 @@
                 dma, dma, dma, dma, dma((2,)), dma((2,)), dma((2,)),
             ],
             compiler_params=pltpu.CompilerParams(
-                collective_id=0, has_side_effects=True, vmem_limit_bytes=60 << 20
+                collective_id=0, has_side_effects=True, vmem_limit_bytes=48 << 20
             ),
             name="balance",
-        )(thickness, labels, outlet, sat_new, sat_old, porosity, spec_storage, pressure, conduct, et_rate)
+        )(*(
+            pltpu.with_memory_space_constraint(v, pltpu.HBM)
+            for v in (thickness, labels, outlet, sat_new, sat_old, porosity, spec_storage, pressure, conduct, et_rate)
+        ))
         return out.reshape(4, layers, SUB), bal, top.reshape(())
 
     cells = P(None, "gx", "gy")

time: 48.6 us -> 43.8 us (0.901)
  Pallas kernels: 42.5 us -> 39.8 us
  local copies, waits for them, and re-layouts: 3.44 us -> 1.45 us
    pallas_call x1, Pallas kernels: 42.5 us -> 39.8 us  [on_device(): pl.pallas_call(make_kernel(ngx, ngy, scale), out_shape=(jax.ShapeDtypeStr...]
    unnamed x2, local copies, waits for them, and re-layouts: 3.44 us -> 1.45 us
where the time goes in v2:
time: 43.8 us; the launch traced here: 43.6 us
  Pallas kernels  39.8 us (91%)
  between operations  2.33 us (5%)
  local copies, waits for them, and re-layouts  1.45 us (3%)
    pallas_call x1, Pallas kernels, on_device(): pl.pallas_call(make_kernel(ngx, ngy, scale), out_shape=(jax.ShapeDtypeStr...  39.8 us
    unnamed x2, local copies, waits for them, and re-layouts  1.45 us

profile of v2, /device:TPU:1, one launch (start us, length us, event | category | flops | bytes accessed | tf_op | source)
XLA Modules:
  0.0 43.6 jit_solution(16453676885537923583)
XLA Ops:
  0.6 39.8 %balance.1 = (f32[256,512]{1,0:T(8,128)S(1)}, f32[4,64,128]{2,1,0:T(8,128)S(1)}, f32[1]{0:T(128)}) custom-call(f32[64]{0:T(128)} %thick_h.1, s32[64,128]{1,0:T(8,128)} %labels_h.1, s32[64,128]{1,0:T(8,128)} %outlet_h.1, f32[64,64,128]{2,1,0:T(8,128)} %sn_h.1, f32[64,64,128]{2,1,0:T(8,128)} %so_h.1, f32[64,64,128]{2,1,0:T(8,128)} %po_h.1, ...), custom_call_target="tpu_custom_call" | custom-call | tf_op jit(solution)/shard_map/balance/pallas_call | solution.py:329
  40.5 0.8 %copy.16 = f32[4,64,512]{2,1,0:T(8,128)} copy(f32[4,64,512]{2,1,0:T(8,128)S(1)} %bitcast.2) | data formatting | bytes 1048576
  41.3 0.7 %copy.17 = f32[4,64,128]{2,1,0:T(8,128)} copy(f32[4,64,128]{2,1,0:T(8,128)S(1)} %get-tuple-element.13) | data formatting | bytes 262144

commit v3 on v2

--- a/solution.py
+++ b/solution.py
@@ -8,10 +8,10 @@
 SUB = 512
 NP = 4
 ZB = 16
+PARTS = (8, 24, 32)
 MESH = pl.DeviceIdType.MESH
 BF = jnp.bfloat16
 F32 = jnp.float32
-NT = (((1,), (1,)), ((), ()))
 
 
 def split(f):
@@ -35,13 +35,14 @@
         thick_h, labels_h, outlet_h, sn_h, so_h, po_h, ss_h, p_h, k_h, et_h,
         out, bal_h, top,
         thick, labels, outlet, sn, so, po, ss, et, p, k, depth, g, a0, a1, oh0, oh1, tot, half, bal,
-        edge, halo, peak, peaks_y, peaks_x, pieces, own,
+        edge, halo, peak, peak_y, peaks_y, peaks_x, pieces, own,
         sem_small, sem_pk, sem_rest, halo_send, halo_recv, pair_send, pair_recv,
-        rs_send, rs_recv, ag_send, ag_recv, pk_send, pk_recv, sem_out,
+        rs_send, rs_recv, ag_send, ag_recv, pk_send, pk_recv, sem_out, main, edges,
     ):
         layers, cx, cy = sn_h.shape
         per = 2 * NP
         turns = cx // per
+        early = turns // 2
         gx = lax.axis_index("gx")
         gy = lax.axis_index("gy")
         chip = gy // 2
@@ -66,29 +67,38 @@
         def greet(to):
             pl.semaphore_signal(barrier, inc=1, device_id=to, device_id_type=MESH)
 
+        smalls = ((thick_h, thick), (labels_h, labels), (outlet_h, outlet))
+        for i, (src, dst) in enumerate(smalls):
+            pltpu.make_async_copy(src, dst, sem_small.at[i]).start()
+
+        for i, (src, dst) in enumerate(((p_h, p), (k_h, k))):
+
+            @pl.loop(0, layers // 4)
+            def _(t, i=i, src=src, dst=dst):
+                for r in range(4):
+                    z = t * 4 + r
+                    pltpu.make_async_copy(src.at[z], dst.at[pl.ds(0, cx), z, :], sem_pk.at[i]).start()
+
         partner = (gx, chip * 2 + 1 - core)
         greet(partner)
         each_chip(lambda i, x, z: greet((x, z * 2 + core)))
         for d in range(1, chips_y):
             greet((gx, chips[d] * 2 + 1 - core))
 
-        smalls = ((thick_h, thick), (labels_h, labels), (outlet_h, outlet))
-        for i, (src, dst) in enumerate(smalls):
-            pltpu.make_async_copy(src, dst, sem_small.at[i]).start()
-
-        @pl.loop(0, layers)
-        def _(z):
-            for i, (src, dst) in enumerate(((p_h, p), (k_h, k))):
-                pltpu.make_async_copy(src.at[z], dst.at[pl.ds(0, cx), z, :], sem_pk.at[i]).start()
-
         rest = ((sn_h, sn), (so_h, so), (po_h, po), (ss_h, ss), (et_h, et))
 
-        @pl.loop(0, turns)
-        def _(c):
-            for r in range(per):
+        @pl.loop(0, PARTS[0])
+        def _(x):
+            for i, (src, dst) in enumerate(rest):
+                pltpu.make_async_copy(src.at[:, x, :], dst.at[x], sem_rest.at[i, 0]).start()
+
+        for part in range(1, len(PARTS)):
+            rows_x = pl.ds(sum(PARTS[:part]), PARTS[part])
+
+            @pl.loop(0, layers)
+            def _(z, part=part, rows_x=rows_x):
                 for i, (src, dst) in enumerate(rest):
-                    x = c * per + r
-                    pltpu.make_async_copy(src.at[:, x, :], dst.at[x], sem_rest.at[i, c]).start()
+                    pltpu.make_async_copy(src.at[z, rows_x, :], dst.at[rows_x, z, :], sem_rest.at[i, part]).start()
 
         for (src, dst), i in zip(smalls, range(3)):
             pltpu.make_async_copy(src, dst, sem_small.at[i]).wait()
@@ -98,46 +108,35 @@
         k[cx] = jnp.zeros((layers, cy), F32)
         g[...] = jnp.zeros_like(g)
         peak[...] = jnp.zeros_like(peak)
-        tot[...] = jnp.zeros_like(tot)
         a1[...] = jnp.zeros_like(a1)
         oh1[...] = jnp.zeros_like(oh1)
-        lane = lax.broadcasted_iota(jnp.int32, (ZB, cy), 1)
-        inner = lane > 0
         iota = lax.broadcasted_iota(jnp.int32, (256, cy), 0).astype(F32).astype(BF)
-        one = jnp.ones((16, cy), BF)
         zero = jnp.zeros((16, cy), BF)
 
         def write_onehot(oh, lab, col):
             high = lab >= 256
             low = jnp.where(high, lab - 256, lab).astype(F32)
             low = jnp.broadcast_to(low, (16, cy)).astype(BF)
-            high = jnp.broadcast_to(jnp.where(high, 1.0, 0.0), (16, cy)).astype(BF)
+            lower = jnp.broadcast_to(jnp.where(high, 0.0, 1.0), (16, cy)).astype(BF)
+            upper = jnp.broadcast_to(jnp.where(high, 1.0, 0.0), (16, cy)).astype(BF)
             for r in range(16):
-                e = jnp.where(iota[r * 16 : (r + 1) * 16] == low, one, zero)
-                eh = e * high
-                oh[r * 16 : r * 16 + 16, col] = e - eh
-                oh[256 + r * 16 : 272 + r * 16, col] = eh
-
-        wait_all(p.at[pl.ds(0, cx)], sem_pk.at[0])
-        wait_all(k.at[pl.ds(0, cx)], sem_pk.at[1])
+                hit = iota[r * 16 : (r + 1) * 16] == low
+                oh[r * 16 : r * 16 + 16, col] = jnp.where(hit, lower, zero)
+                oh[256 + r * 16 : 272 + r * 16, col] = jnp.where(hit, upper, zero)
 
         lanes = lax.broadcasted_iota(jnp.int32, (layers, cy), 1)
-
-        def take(t, carry):
-            for x in (4 * t, 4 * t + 1, 4 * t + 2, 4 * t + 3):
-                first, last = lanes == x, lanes == x + cx
-                res = []
-                for ref, acc in zip((p, k), carry):
+        for i, ref in enumerate((p, k)):
+            wait_all(ref.at[pl.ds(0, cx)], sem_pk.at[i])
+
+            def take(t, acc, ref=ref):
+                for r in range(8):
+                    x = t * 8 + r
                     v = ref[x]
-                    acc = jnp.where(first, pltpu.roll(v, x, 1), acc)
-                    res.append(jnp.where(last, pltpu.roll(v, x + cx + 1, 1), acc))
-                carry = tuple(res)
-            return carry
-
-        e0 = jnp.zeros((layers, cy), F32)
-        ep, ek = lax.fori_loop(0, cx // 4, take, (e0, e0))
-        edge[0] = ep
-        edge[1] = ek
+                    acc = jnp.where(lanes == x, pltpu.roll(v, x, 1), acc)
+                    acc = jnp.where(lanes == x + cx, pltpu.roll(v, x + cx + 1, 1), acc)
+                return acc
+
+            edge[i] = lax.fori_loop(0, cx // 8, take, jnp.zeros((layers, cy), F32))
 
         def fields(x, a, oh, j):
             col = slice(j * cy, (j + 1) * cy)
@@ -153,7 +152,6 @@
                 gp = g[zs, :]
                 g[zs, :] = gn
                 h = face_flow(pc, kc, pltpu.roll(pc, 1, 1), pltpu.roll(kc, 1, 1))
-                h = jnp.where(inner, h, 0.0)
                 flux = (d + d) * (gp - gn + h - pltpu.roll(h, cy - 1, 1))
                 snv, pov = sn[x, zs, :], po[x, zs, :]
                 dif = snv - so[x, zs, :]
@@ -172,19 +170,33 @@
             for q in range(4):
                 bal[q, pl.ds(x, 1), :] = jnp.sum(sums[q], axis=0, keepdims=True)
 
-        def product(a, oh):
-            r = lax.dot_general(a[...], oh[...], NT, preferred_element_type=F32)
-            tot[...] += r[: 4 * layers] + r[4 * layers :]
+        def product(a, oh, rows, sums, width):
+            for t in range(width // 256):
+                col = slice(t * 256, t * 256 + 256)
+                for m in (0, 1):
+                    pltpu.matmul_push_rhs(
+                        oh[m * 256 : m * 256 + 256, col], staging_register=t % 2, mxu_index=m, transpose=True
+                    )
+                for m in (0, 1):
+                    pltpu.matmul_acc_lhs(sums[m], a[:rows, col], load_staged_rhs=t % 2)
+                    pltpu.matmul_acc_lhs(sums[m], a[rows : 2 * rows, col])
 
         def turns_of(begin, end):
             @pl.loop(begin, end)
             def _(c):
-                for i, (_, dst) in enumerate(rest):
-                    wait_all(dst.at[pl.ds(c * per, per)], sem_rest.at[i, c])
-                product(a1, oh1)
+                for part, size in enumerate(PARTS):
+                    begin_x = sum(PARTS[:part])
+                    if begin <= begin_x // per < end:
+
+                        @pl.when(c == begin_x // per)
+                        def _(part=part, size=size, begin_x=begin_x):
+                            for i, (_, dst) in enumerate(rest):
+                                wait_all(dst.at[pl.ds(begin_x, size)], sem_rest.at[i, part])
+
+                product(a1, oh1, 4 * layers, main, NP * cy)
                 for j in range(NP):
                     fields(c * per + j, a0, oh0, j)
-                product(a0, oh0)
+                product(a0, oh0, 4 * layers, main, NP * cy)
                 for j in range(NP):
                     fields(c * per + NP + j, a1, oh1, j)
 
@@ -195,7 +207,7 @@
             copy.start()
             return copy
 
-        turns_of(0, turns // 2)
+        turns_of(0, early)
         pl.semaphore_wait(barrier, (ngx + 1) * chips_y - 1)
 
         x_next, x_last = wrap(gx + 1, ngx), wrap(gx + ngx - 1, ngx)
@@ -210,15 +222,17 @@
             ):
                 halos.append(send(src, halo.at[slot], halo_send.at[slot], halo_recv.at[slot], to))
 
-        turns_of(turns // 2, turns)
-        product(a1, oh1)
-
-        chips8 = [wrap(gy + d, ngy) for d in range(1, ngy)]
-        for d in range(ngy - 1):
-            send(peak, peaks_y.at[d], pk_send.at[0], pk_recv.at[0], (gx, chips8[d]))
+        turns_of(early, turns)
+
+        peak[...] = jnp.broadcast_to(jnp.max(peak[...], axis=0, keepdims=True), (8, cy))
+
+        @pl.loop(1, ngx)
+        def _(d):
+            send(peak.at[:1, :], peaks_x.at[d - 1], pk_send.at[0], pk_recv.at[0], (wrap(gx + d, ngx), gy))
 
         for h in halos:
             h.wait()
+        product(a1, oh1, 4 * layers, main, NP * cy)
         left = lanes < cx
         ly = jnp.concatenate([labels[...]] * 2, axis=0).astype(F32).T
         oy = jnp.concatenate([outlet[...]] * 2, axis=0).astype(F32).T
@@ -238,7 +252,10 @@
             (edge[0], edge[1], py, ky * inside, lab_y, out_y),
         )
         for i, (pc, kc, pn, kn, lab, mask) in enumerate(borders):
-            f = d2 * face_flow(pc, kc, pn, kn)
+            f = face_flow(pc, kc, pn, kn)
+            if i == 2:
+                f = f - face_flow(pc, kc, pltpu.roll(pc, cx, 1), pltpu.roll(kc, cx, 1))
+            f = d2 * f
             col = slice(i * cy, (i + 1) * cy)
             write_onehot(oh0, lab, col)
             high, low = split(f * mask)
@@ -254,10 +271,13 @@
                 low_side = jnp.where(at == 0, jnp.broadcast_to(ft[:cx, :1], (cx, cy)), 0.0)
                 high_side = jnp.where(at == cy - 1, jnp.broadcast_to(ft[cx:, :1], (cx, cy)), 0.0)
                 bal[3] += low_side + high_side
-        r = lax.dot_general(
-            a0[: 2 * layers, : 3 * cy], oh0[:, : 3 * cy], NT, preferred_element_type=F32
-        )
-        tot[pl.ds(3 * layers, layers), :] += r[:layers] + r[layers:]
+        a0[: 2 * layers, 3 * cy : 4 * cy] = jnp.zeros((2 * layers, cy), BF)
+        product(a0, oh0, layers, edges, 4 * cy)
+        for m in (0, 1):
+            col = slice(m * 256, m * 256 + 256)
+            r = pltpu.matmul_pop(main[m])
+            tot[: 3 * layers, col] = r[: 3 * layers]
+            tot[3 * layers :, col] = r[3 * layers :] + pltpu.matmul_pop(edges[m])
 
         rows = 2 * layers
         mine, theirs = (pl.multiple_of(v * rows, rows) for v in (core, 1 - core))
@@ -265,13 +285,6 @@
         bal_copy = pltpu.make_async_copy(bal, bal_h, sem_out.at[0])
         bal_copy.start()
 
-        wait_all(peaks_y, pk_recv.at[0])
-        wait_all(peaks_y, pk_send.at[0])
-        best = peak[...]
-        for d in range(ngy - 1):
-            best = jnp.maximum(best, peaks_y[d])
-        peak[...] = best
-
         pair.wait()
         tot[pl.ds(mine, rows), :] += half[...]
 
@@ -281,10 +294,6 @@
             ]
 
         each_chip(lambda i, x, z: send(tile(tot, x, z), pieces.at[i], rs_send, rs_recv, (x, z * 2 + core)))
-
-        @pl.loop(1, ngx)
-        def _(d):
-            send(peak, peaks_x.at[d - 1], pk_send.at[1], pk_recv.at[1], (wrap(gx + d, ngx), gy))
 
         wait_all(pieces, rs_recv)
         terms = [tile(tot, gx, chip)[...]] + [pieces[d] for d in range(n // 2 - 1)]
@@ -296,12 +305,14 @@
         each_chip(lambda i, x, z: send(own, here, ag_send, ag_recv, (x, z * 2 + core)))
         own_copy = pltpu.make_async_copy(own, here, sem_out.at[1])
         own_copy.start()
-        wait_all(peaks_x, pk_recv.at[1])
-        wait_all(peaks_x, pk_send.at[1])
-        best = peak[...]
+        wait_all(peaks_x, pk_recv.at[0])
+        wait_all(peaks_x, pk_send.at[0])
+        best = peak[:1, :]
         for d in range(ngx - 1):
             best = jnp.maximum(best, peaks_x[d])
-        top[0] = jnp.max(best)
+        peak_y[...] = best
+        for d in range(1, ngy):
+            send(peak_y, peaks_y.at[d - 1], pk_send.at[1], pk_recv.at[1], (gx, wrap(gy + d, ngy)))
         bal_copy.wait()
         wait_all(pieces, rs_send)
         wait_all(pieces, ag_recv)
@@ -309,9 +320,28 @@
         done = out.at[pl.ds(mine, rows), :]
         pair = send(done, done, pair_send.at[1], pair_recv.at[1], partner)
         wait_all(pieces, ag_send)
+        wait_all(peaks_y, pk_recv.at[1])
+        wait_all(peaks_y, pk_send.at[1])
+        for d in range(ngy - 1):
+            best = jnp.maximum(best, peaks_y[d])
+        top[0] = jnp.max(best)
         pair.wait()
 
-    return kernel
+    def with_sums(*refs):
+        layers = refs[3].shape[0]
+
+        def body(main_0, main_1, edge_0, edge_1):
+            for r in (main_0, main_1, edge_0, edge_1):
+                pltpu.matmul_pop(r)
+            kernel(*refs, (main_0, main_1), (edge_0, edge_1))
+
+        pl.run_scoped(
+            body,
+            pltpu.ACC(0)((4 * layers, 256), F32), pltpu.ACC(1)((4 * layers, 256), F32),
+            pltpu.ACC(0)((layers, 256), F32), pltpu.ACC(1)((layers, 256), F32),
+        )
+
+    return with_sums
 
 
 def solution(mesh):
@@ -352,11 +382,12 @@
                 pltpu.VMEM((2, layers, cy), F32),
                 pltpu.VMEM((8, layers, cy), F32),
                 pltpu.VMEM((8, cy), F32),
-                pltpu.VMEM((ngy - 1, 8, cy), F32),
-                pltpu.VMEM((ngx - 1, 8, cy), F32),
+                pltpu.VMEM((1, cy), F32),
+                pltpu.VMEM((ngy - 1, 1, cy), F32),
+                pltpu.VMEM((ngx - 1, 1, cy), F32),
                 pltpu.VMEM((n // 2 - 1, 8, 128), F32),
                 pltpu.VMEM((8, 128), F32),
-                dma((3,)), dma((2,)), dma((5, cx // (2 * NP))), dma((8,)), dma((8,)), dma((2,)), dma((2,)),
+                dma((3,)), dma((2,)), dma((5, len(PARTS))), dma((8,)), dma((8,)), dma((2,)), dma((2,)),
                 dma, dma, dma, dma, dma((2,)), dma((2,)), dma((2,)),
             ],
             compiler_params=pltpu.CompilerParams(

time: 43.8 us -> 43.4 us (level)
  no operation moved by 1% of the time
where the time goes in v3:
time: 43.4 us; the launch traced here: 43.3 us
  Pallas kernels  39.5 us (91%)
  between operations  2.33 us (5%)
  local copies, waits for them, and re-layouts  1.45 us (3%)
    pallas_call x1, Pallas kernels, on_device(): pl.pallas_call(make_kernel(ngx, ngy, scale), out_shape=(jax.ShapeDtypeStr...  39.5 us
    unnamed x2, local copies, waits for them, and re-layouts  1.45 us

profile of v3, /device:TPU:1, one launch (start us, length us, event | category | flops | bytes accessed | tf_op | source)
XLA Modules:
  0.0 43.3 jit_solution(4901836348983059267)
XLA Ops:
  0.6 39.5 %balance.1 = (f32[256,512]{1,0:T(8,128)S(1)}, f32[4,64,128]{2,1,0:T(8,128)S(1)}, f32[1]{0:T(128)}) custom-call(f32[64]{0:T(128)} %refs_0_.1, s32[64,128]{1,0:T(8,128)} %refs_1_.1, s32[64,128]{1,0:T(8,128)} %refs_2_.1, f32[64,64,128]{2,1,0:T(8,128)} %refs_3_.1, f32[64,64,128]{2,1,0:T(8,128)} %refs_4_.1, f32[64,64,128]{2,1,0:T(8,128)} %refs_5_.1, ...), custom_call_target="tpu_custom_call" | custom-call | tf_op jit(solution)/shard_map/balance/pallas_call | solution.py:359
  40.1 0.8 %copy.16 = f32[4,64,512]{2,1,0:T(8,128)} copy(f32[4,64,512]{2,1,0:T(8,128)S(1)} %bitcast.2) | data formatting | bytes 1048576
  40.9 0.7 %copy.17 = f32[4,64,128]{2,1,0:T(8,128)} copy(f32[4,64,128]{2,1,0:T(8,128)S(1)} %get-tuple-element.13) | data formatting | bytes 262144

commit v4 on v3

--- a/solution.py
+++ b/solution.py
@@ -42,7 +42,7 @@
         layers, cx, cy = sn_h.shape
         per = 2 * NP
         turns = cx // per
-        early = turns // 2
+        early = turns * 3 // 8
         gx = lax.axis_index("gx")
         gy = lax.axis_index("gy")
         chip = gy // 2
@@ -55,14 +55,18 @@
         chips = [wrap(chip + d, chips_y) for d in range(chips_y)]
 
         def each_chip(f):
+            order = sorted(range(chips_y), key=lambda d: -min(d, chips_y - d))
+            far = ngx * 3 // 8
+            for begin, end in ((far, ngx), (1, far)):
+
+                @pl.loop(begin, end)
+                def _(i):
+                    at = wrap(gx + i, ngx)
+                    for d in order:
+                        f(i * chips_y + d - 1, at, chips[d])
+
             for d in range(1, chips_y):
                 f(d - 1, gx, chips[d])
-
-            @pl.loop(1, ngx)
-            def _(i):
-                at = wrap(gx + i, ngx)
-                for d in range(chips_y):
-                    f(i * chips_y + d - 1, at, chips[d])
 
         def greet(to):
             pl.semaphore_signal(barrier, inc=1, device_id=to, device_id_type=MESH)
@@ -73,11 +77,17 @@
 
         for i, (src, dst) in enumerate(((p_h, p), (k_h, k))):
 
-            @pl.loop(0, layers // 4)
+            @pl.loop(0, layers // 16)
             def _(t, i=i, src=src, dst=dst):
-                for r in range(4):
-                    z = t * 4 + r
+                for r in range(16):
+                    z = t * 16 + r
                     pltpu.make_async_copy(src.at[z], dst.at[pl.ds(0, cx), z, :], sem_pk.at[i]).start()
+
+        rest = ((sn_h, sn), (so_h, so), (po_h, po), (ss_h, ss), (et_h, et))
+
+        for x in range(PARTS[0]):
+            for i, (src, dst) in enumerate(rest):
+                pltpu.make_async_copy(src.at[:, x, :], dst.at[x], sem_rest.at[i, 0]).start()
 
         partner = (gx, chip * 2 + 1 - core)
         greet(partner)
@@ -85,20 +95,15 @@
         for d in range(1, chips_y):
             greet((gx, chips[d] * 2 + 1 - core))
 
-        rest = ((sn_h, sn), (so_h, so), (po_h, po), (ss_h, ss), (et_h, et))
-
-        @pl.loop(0, PARTS[0])
-        def _(x):
-            for i, (src, dst) in enumerate(rest):
-                pltpu.make_async_copy(src.at[:, x, :], dst.at[x], sem_rest.at[i, 0]).start()
-
         for part in range(1, len(PARTS)):
             rows_x = pl.ds(sum(PARTS[:part]), PARTS[part])
 
-            @pl.loop(0, layers)
-            def _(z, part=part, rows_x=rows_x):
-                for i, (src, dst) in enumerate(rest):
-                    pltpu.make_async_copy(src.at[z, rows_x, :], dst.at[rows_x, z, :], sem_rest.at[i, part]).start()
+            @pl.loop(0, layers // 8)
+            def _(t, part=part, rows_x=rows_x):
+                for r in range(8):
+                    z = t * 8 + r
+                    for i, (src, dst) in enumerate(rest):
+                        pltpu.make_async_copy(src.at[z, rows_x, :], dst.at[rows_x, z, :], sem_rest.at[i, part]).start()
 
         for (src, dst), i in zip(smalls, range(3)):
             pltpu.make_async_copy(src, dst, sem_small.at[i]).wait()
@@ -128,15 +133,17 @@
         for i, ref in enumerate((p, k)):
             wait_all(ref.at[pl.ds(0, cx)], sem_pk.at[i])
 
-            def take(t, acc, ref=ref):
+            def take(t, carry, ref=ref):
+                low, high = carry
                 for r in range(8):
                     x = t * 8 + r
-                    v = ref[x]
-                    acc = jnp.where(lanes == x, pltpu.roll(v, x, 1), acc)
-                    acc = jnp.where(lanes == x + cx, pltpu.roll(v, x + cx + 1, 1), acc)
-                return acc
-
-            edge[i] = lax.fori_loop(0, cx // 8, take, jnp.zeros((layers, cy), F32))
+                    v = pltpu.roll(ref[x], x + cx, 1)
+                    low = jnp.where(lanes == x + cx, v, low)
+                    high = jnp.where(lanes == x + cx - 1, v, high)
+                return low, high
+
+            low, high = lax.fori_loop(0, cx // 8, take, (jnp.zeros((layers, cy), F32),) * 2)
+            edge[i] = jnp.where(lanes < cx, pltpu.roll(low, cx, 1), pltpu.roll(high, 1, 1))
 
         def fields(x, a, oh, j):
             col = slice(j * cy, (j + 1) * cy)

time: 43.4 us -> 40.8 us (0.940)
  Pallas kernels: 39.5 us -> 36.9 us
    pallas_call x1, Pallas kernels: 39.5 us -> 36.9 us  [on_device(): pl.pallas_call(make_kernel(ngx, ngy, scale), out_shape=(jax.ShapeDtypeStr...]
where the time goes in v4:
time: 40.8 us; the launch traced here: 40.7 us
  Pallas kernels  36.9 us (90%)
  between operations  2.33 us (6%)
  local copies, waits for them, and re-layouts  1.45 us (4%)
    pallas_call x1, Pallas kernels, on_device(): pl.pallas_call(make_kernel(ngx, ngy, scale), out_shape=(jax.ShapeDtypeStr...  36.9 us
    unnamed x2, local copies, waits for them, and re-layouts  1.45 us

profile of v4, /device:TPU:1, one launch (start us, length us, event | category | flops | bytes accessed | tf_op | source)
XLA Modules:
  0.0 40.7 jit_solution(16510625389380379816)
XLA Ops:
  0.6 36.9 %balance.1 = (f32[256,512]{1,0:T(8,128)S(1)}, f32[4,64,128]{2,1,0:T(8,128)S(1)}, f32[1]{0:T(128)}) custom-call(f32[64]{0:T(128)} %refs_0_.1, s32[64,128]{1,0:T(8,128)} %refs_1_.1, s32[64,128]{1,0:T(8,128)} %refs_2_.1, f32[64,64,128]{2,1,0:T(8,128)} %refs_3_.1, f32[64,64,128]{2,1,0:T(8,128)} %refs_4_.1, f32[64,64,128]{2,1,0:T(8,128)} %refs_5_.1, ...), custom_call_target="tpu_custom_call" | custom-call | tf_op jit(solution)/shard_map/balance/pallas_call | solution.py:366
  37.6 0.8 %copy.16 = f32[4,64,512]{2,1,0:T(8,128)} copy(f32[4,64,512]{2,1,0:T(8,128)S(1)} %bitcast.2) | data formatting | bytes 1048576
  38.4 0.7 %copy.17 = f32[4,64,128]{2,1,0:T(8,128)} copy(f32[4,64,128]{2,1,0:T(8,128)S(1)} %get-tuple-element.13) | data formatting | bytes 262144

commit v5 on v4

--- a/solution.py
+++ b/solution.py
@@ -42,7 +42,7 @@
         layers, cx, cy = sn_h.shape
         per = 2 * NP
         turns = cx // per
-        early = turns * 3 // 8
+        early = turns * 2 // 8
         gx = lax.axis_index("gx")
         gy = lax.axis_index("gy")
         chip = gy // 2
@@ -54,8 +54,9 @@
 
         chips = [wrap(chip + d, chips_y) for d in range(chips_y)]
 
+        order = sorted(range(chips_y), key=lambda d: -min(d, chips_y - d))
+
         def each_chip(f):
-            order = sorted(range(chips_y), key=lambda d: -min(d, chips_y - d))
             far = ngx * 3 // 8
             for begin, end in ((far, ngx), (1, far)):
 
@@ -63,10 +64,10 @@
                 def _(i):
                     at = wrap(gx + i, ngx)
                     for d in order:
-                        f(i * chips_y + d - 1, at, chips[d])
+                        f(i * chips_y + d - 1, at, chips[d], d)
 
             for d in range(1, chips_y):
-                f(d - 1, gx, chips[d])
+                f(d - 1, gx, chips[d], d)
 
         def greet(to):
             pl.semaphore_signal(barrier, inc=1, device_id=to, device_id_type=MESH)
@@ -91,7 +92,7 @@
 
         partner = (gx, chip * 2 + 1 - core)
         greet(partner)
-        each_chip(lambda i, x, z: greet((x, z * 2 + core)))
+        each_chip(lambda i, x, z, d: greet((x, z * 2 + core)))
         for d in range(1, chips_y):
             greet((gx, chips[d] * 2 + 1 - core))
 
@@ -300,7 +301,7 @@
                 pl.ds(pl.multiple_of(core * rows + x * 8, 8), 8), pl.ds(pl.multiple_of(z * 128, 128), 128)
             ]
 
-        each_chip(lambda i, x, z: send(tile(tot, x, z), pieces.at[i], rs_send, rs_recv, (x, z * 2 + core)))
+        each_chip(lambda i, x, z, d: send(tile(tot, x, z), pieces.at[i], rs_send, rs_recv, (x, z * 2 + core)))
 
         wait_all(pieces, rs_recv)
         terms = [tile(tot, gx, chip)[...]] + [pieces[d] for d in range(n // 2 - 1)]
@@ -309,7 +310,7 @@
         own[...] = terms[0] * scale
 
         here = tile(out, gx, chip)
-        each_chip(lambda i, x, z: send(own, here, ag_send, ag_recv, (x, z * 2 + core)))
+        each_chip(lambda i, x, z, d: send(own, here, ag_send, ag_recv.at[d], (x, z * 2 + core)))
         own_copy = pltpu.make_async_copy(own, here, sem_out.at[1])
         own_copy.start()
         wait_all(peaks_x, pk_recv.at[0])
@@ -322,17 +323,21 @@
             send(peak_y, peaks_y.at[d - 1], pk_send.at[1], pk_recv.at[1], (gx, wrap(gy + d, ngy)))
         bal_copy.wait()
         wait_all(pieces, rs_send)
-        wait_all(pieces, ag_recv)
         own_copy.wait()
-        done = out.at[pl.ds(mine, rows), :]
-        pair = send(done, done, pair_send.at[1], pair_recv.at[1], partner)
+        passed = []
+        for d in reversed(order):
+            wait_all(pieces.at[pl.ds(0, ngx - (d == 0))], ag_recv.at[d])
+            source = wrap(chip + chips_y - d, chips_y)
+            block = out.at[pl.ds(mine, rows), pl.ds(pl.multiple_of(source * 128, 128), 128)]
+            passed.append(send(block, block, pair_send.at[1 + d], pair_recv.at[1 + d], partner))
         wait_all(pieces, ag_send)
         wait_all(peaks_y, pk_recv.at[1])
         wait_all(peaks_y, pk_send.at[1])
         for d in range(ngy - 1):
             best = jnp.maximum(best, peaks_y[d])
         top[0] = jnp.max(best)
-        pair.wait()
+        for copy in passed:
+            copy.wait()
 
     def with_sums(*refs):
         layers = refs[3].shape[0]
@@ -394,8 +399,8 @@
                 pltpu.VMEM((ngx - 1, 1, cy), F32),
                 pltpu.VMEM((n // 2 - 1, 8, 128), F32),
                 pltpu.VMEM((8, 128), F32),
-                dma((3,)), dma((2,)), dma((5, len(PARTS))), dma((8,)), dma((8,)), dma((2,)), dma((2,)),
-                dma, dma, dma, dma, dma((2,)), dma((2,)), dma((2,)),
+                dma((3,)), dma((2,)), dma((5, len(PARTS))), dma((8,)), dma((8,)), dma((1 + ngy // 2,)), dma((1 + ngy // 2,)),
+                dma, dma, dma, dma((ngy // 2,)), dma((2,)), dma((2,)), dma((2,)),
             ],
             compiler_params=pltpu.CompilerParams(
                 collective_id=0, has_side_effects=True, vmem_limit_bytes=48 << 20

time: 40.8 us -> 39.9 us (0.978)
  Pallas kernels: 36.9 us -> 36 us
    pallas_call x1, Pallas kernels: 36.9 us -> 36 us  [on_device(): pl.pallas_call(make_kernel(ngx, ngy, scale), out_shape=(jax.ShapeDtypeStr...]
where the time goes in v5:
time: 39.9 us; the launch traced here: 39.8 us
  Pallas kernels  36 us (90%)
  between operations  2.33 us (6%)
  local copies, waits for them, and re-layouts  1.45 us (4%)
    pallas_call x1, Pallas kernels, on_device(): pl.pallas_call(make_kernel(ngx, ngy, scale), out_shape=(jax.ShapeDtypeStr...  36 us
    unnamed x2, local copies, waits for them, and re-layouts  1.45 us

profile of v5, /device:TPU:1, one launch (start us, length us, event | category | flops | bytes accessed | tf_op | source)
XLA Modules:
  0.0 39.8 jit_solution(10203880010255027057)
XLA Ops:
  0.6 36.0 %balance.1 = (f32[256,512]{1,0:T(8,128)S(1)}, f32[4,64,128]{2,1,0:T(8,128)S(1)}, f32[1]{0:T(128)}) custom-call(f32[64]{0:T(128)} %refs_0_.1, s32[64,128]{1,0:T(8,128)} %refs_1_.1, s32[64,128]{1,0:T(8,128)} %refs_2_.1, f32[64,64,128]{2,1,0:T(8,128)} %refs_3_.1, f32[64,64,128]{2,1,0:T(8,128)} %refs_4_.1, f32[64,64,128]{2,1,0:T(8,128)} %refs_5_.1, ...), custom_call_target="tpu_custom_call" | custom-call | tf_op jit(solution)/shard_map/balance/pallas_call | solution.py:371
  36.7 0.8 %copy.16 = f32[4,64,512]{2,1,0:T(8,128)} copy(f32[4,64,512]{2,1,0:T(8,128)S(1)} %bitcast.2) | data formatting | bytes 1048576
  37.5 0.7 %copy.17 = f32[4,64,128]{2,1,0:T(8,128)} copy(f32[4,64,128]{2,1,0:T(8,128)S(1)} %get-tuple-element.13) | data formatting | bytes 262144

commit v6 on v5

--- a/solution.py
+++ b/solution.py
@@ -231,12 +231,6 @@
                 halos.append(send(src, halo.at[slot], halo_send.at[slot], halo_recv.at[slot], to))
 
         turns_of(early, turns)
-
-        peak[...] = jnp.broadcast_to(jnp.max(peak[...], axis=0, keepdims=True), (8, cy))
-
-        @pl.loop(1, ngx)
-        def _(d):
-            send(peak.at[:1, :], peaks_x.at[d - 1], pk_send.at[0], pk_recv.at[0], (wrap(gx + d, ngx), gy))
 
         for h in halos:
             h.wait()
@@ -292,6 +286,13 @@
         pair = send(tot.at[pl.ds(theirs, rows), :], half, pair_send.at[0], pair_recv.at[0], partner)
         bal_copy = pltpu.make_async_copy(bal, bal_h, sem_out.at[0])
         bal_copy.start()
+
+        peak[...] = jnp.broadcast_to(jnp.max(peak[...], axis=0, keepdims=True), (8, cy))
+
+        @pl.loop(1, ngx)
+        def _(d):
+            send(peak.at[:1, :], peaks_x.at[d - 1], pk_send.at[0], pk_recv.at[0], (wrap(gx + d, ngx), gy))
+
 
         pair.wait()
         tot[pl.ds(mine, rows), :] += half[...]

time: 39.9 us -> 39.9 us (level)
  no operation moved by 1% of the time
where the time goes in v6:
time: 39.9 us; the launch traced here: 39.7 us
  Pallas kernels  36 us (90%)
  between operations  2.33 us (6%)
  local copies, waits for them, and re-layouts  1.45 us (4%)
    pallas_call x1, Pallas kernels, on_device(): pl.pallas_call(make_kernel(ngx, ngy, scale), out_shape=(jax.ShapeDtypeStr...  36 us
    unnamed x2, local copies, waits for them, and re-layouts  1.45 us

profile of v6, /device:TPU:1, one launch (start us, length us, event | category | flops | bytes accessed | tf_op | source)
XLA Modules:
  0.0 39.7 jit_solution(5221005825249861373)
XLA Ops:
  0.6 36.0 %balance.1 = (f32[256,512]{1,0:T(8,128)S(1)}, f32[4,64,128]{2,1,0:T(8,128)S(1)}, f32[1]{0:T(128)}) custom-call(f32[64]{0:T(128)} %refs_0_.1, s32[64,128]{1,0:T(8,128)} %refs_1_.1, s32[64,128]{1,0:T(8,128)} %refs_2_.1, f32[64,64,128]{2,1,0:T(8,128)} %refs_3_.1, f32[64,64,128]{2,1,0:T(8,128)} %refs_4_.1, f32[64,64,128]{2,1,0:T(8,128)} %refs_5_.1, ...), custom_call_target="tpu_custom_call" | custom-call | tf_op jit(solution)/shard_map/balance/pallas_call | solution.py:372
  36.6 0.8 %copy.16 = f32[4,64,512]{2,1,0:T(8,128)} copy(f32[4,64,512]{2,1,0:T(8,128)S(1)} %bitcast.2) | data formatting | bytes 1048576
  37.4 0.7 %copy.17 = f32[4,64,128]{2,1,0:T(8,128)} copy(f32[4,64,128]{2,1,0:T(8,128)S(1)} %get-tuple-element.13) | data formatting | bytes 262144
